TPU v7x, 32 devices: a whole 2x2x4 slice. The times are simulated.
32 devices in a mesh: lat: 4 (over z), lon: 4 (over y, x), lev: 2 (over core).
Axes of the slice: x: 2, y: 2, z: 4, core: 2. Of those that a mesh axis runs over, the one named last changes fastest.
Arguments:
- pressure: float32 [16, 256, 128, 128], P('lat', 'lon', 'lev'), may hold values from 0.2 to 1.8
- earlier: float32 [16, 256, 128, 128], P('lat', 'lon', 'lev'), may hold values from 0.2 to 1.8
- speed_square: float32 [16, 256, 128, 128], P('lat', 'lon', 'lev'), may hold values from 0.05 to 0.3
Outputs:
- pressure_end: float32 [16, 256, 128, 128], P('lat', 'lon', 'lev')
All inputs are finite; a program needn't handle non-finite values.
Results may differ from a plain program's by a relative error of at most 0.00002.
Values sent between devices are 32-bit elements.
A program may use at most 320 MiB of HBM per device.

v0:
```python
import functools
import math

import jax
import jax.numpy as jnp
from jax import lax
from jax.experimental import pallas as pl
from jax.experimental.pallas import tpu as pltpu
from jax.sharding import PartitionSpec as P

STEPS = 4
CHUNKS = 8
PAD = 8
AXES = ("lat", "lon", "lev")
MESH = pl.DeviceIdType.MESH


def kernel(
    counts,
    chunks,
    start_ref,
    earlier_ref,
    speed_ref,
    end_ref,
    even,
    odd,
    speed,
    load_sem,
    lat_send,
    lat_recv,
    side_send,
    side_recv,
):
    rows, columns, depth, lanes = start_ref.shape
    width = columns // chunks
    fields = (even, odd)
    me = [lax.axis_index(axis) for axis in AXES]
    inside = pl.ds(PAD, depth)
    below = [place > 0 for place in me]
    above = [place < count - 1 for place, count in zip(me, counts)]
    has = [(below[dim], above[dim]) for dim in range(3)]

    edges = (0, rows - 1) if rows > 1 else (0,)
    early = [
        pltpu.make_async_copy(
            start_ref.at[plane, pl.ds(0, width)], even.at[plane + 1, pl.ds(1, width), inside], load_sem.at[place]
        )
        for place, plane in enumerate(edges)
    ]
    loads = [
        pltpu.make_async_copy(earlier_ref, odd.at[pl.ds(1, rows), pl.ds(1, columns), inside], load_sem.at[2]),
        pltpu.make_async_copy(speed_ref, speed, load_sem.at[3]),
    ]
    if chunks > 1:
        loads += [
            pltpu.make_async_copy(
                start_ref.at[plane, pl.ds(width, columns - width)],
                even.at[plane + 1, pl.ds(1 + width, columns - width), inside],
                load_sem.at[4 + place],
            )
            for place, plane in enumerate(edges)
        ]
    if rows > 2:
        loads.append(
            pltpu.make_async_copy(
                start_ref.at[pl.ds(1, rows - 2)],
                even.at[pl.ds(2, rows - 2), pl.ds(1, columns), inside],
                load_sem.at[6],
            )
        )
    for load in early:
        load.start()

    barrier = pltpu.get_barrier_semaphore()
    greeted = jnp.int32(0)
    for dim, axis in enumerate(AXES):
        for side, shift in enumerate((-1, 1)):
            greeted = greeted + has[dim][side].astype(jnp.int32)

            @pl.when(has[dim][side])
            def _():
                pl.semaphore_signal(barrier, inc=1, device_id={axis: me[dim] + shift}, device_id_type=MESH)

    pl.semaphore_wait(barrier, greeted)

    def lat_copy(step, side, chunk, target, held):
        field = fields[step % 2]
        first = chunk * width
        if step == 0 and not held:
            source = start_ref.at[(0, rows - 1)[side], pl.ds(first, width)]
        else:
            source = field.at[(1, rows)[side], pl.ds(first + 1, width), inside]
        return pltpu.make_async_remote_copy(
            src_ref=source,
            dst_ref=field.at[(rows + 1, 0)[side], pl.ds(first + 1, width), inside],
            send_sem=lat_send.at[step % 2, side, chunk],
            recv_sem=lat_recv.at[step % 2, side, chunk],
            device_id={"lat": target},
            device_id_type=MESH,
        )

    def side_copy(step, dim, side, target):
        field = fields[step % 2]
        if dim == 1:
            if step == 0:
                source = start_ref.at[:, (0, columns - 1)[side]]
            else:
                source = field.at[pl.ds(1, rows), (1, columns)[side], inside]
            dest = field.at[pl.ds(1, rows), (columns + 1, 0)[side], inside]
        else:
            if step == 0:
                source = start_ref.at[:, :, pl.ds((0, depth - PAD)[side], PAD)]
            else:
                source = field.at[pl.ds(1, rows), pl.ds(1, columns), pl.ds((PAD, depth)[side], PAD)]
            dest = field.at[pl.ds(1, rows), pl.ds(1, columns), pl.ds((PAD + depth, 0)[side], PAD)]
        return pltpu.make_async_remote_copy(
            src_ref=source,
            dst_ref=dest,
            send_sem=side_send.at[step % 2, dim - 1, side],
            recv_sem=side_recv.at[step % 2, dim - 1, side],
            device_id={AXES[dim]: target},
            device_id_type=MESH,
        )

    def lat_each(step, chunk, act, held=False):
        for side, shift in enumerate((-1, 1)):
            incoming = act == "recv"

            @pl.when(has[0][1 - side if incoming else side])
            def _():
                copy = lat_copy(step, side, chunk, me[0] - shift if incoming else me[0] + shift, held)
                if incoming:
                    copy.wait_recv()
                elif act == "send":
                    copy.wait_send()
                else:
                    copy.start()

    def side_each(step, act):
        for dim in (1, 2):
            for side, shift in enumerate((-1, 1)):
                incoming = act == "recv"

                @pl.when(has[dim][1 - side if incoming else side])
                def _():
                    copy = side_copy(step, dim, side, me[dim] - shift if incoming else me[dim] + shift)
                    if incoming:
                        copy.wait_recv()
                    elif act == "send":
                        copy.wait_send()
                    else:
                        copy.start()

    for load in early:
        load.wait()
    lat_each(0, 0, "start", held=True)

    @pl.loop(1, chunks)
    def _(chunk):
        lat_each(0, chunk, "start")

    side_each(0, "start")
    for load in loads:
        load.start()

    for side in (0, 1):

        @pl.when(jnp.logical_not(has[0][side]))
        def _():
            @pl.loop(1, columns + 1)
            def _(x):
                for field in fields:
                    field[(0, rows + 1)[side], x, inside] = jnp.zeros((depth, lanes), jnp.float32)

        @pl.when(jnp.logical_not(has[1][side]))
        def _():
            for field in fields:
                for y in range(1, rows + 1):
                    field[y, (0, columns + 1)[side], inside] = jnp.zeros((depth, lanes), jnp.float32)

        @pl.when(jnp.logical_not(has[2][side]))
        def _():
            @pl.loop(1, columns + 1)
            def _(x):
                for field in fields:
                    for y in range(1, rows + 1):
                        field[y, x, pl.ds((0, PAD + depth)[side], PAD)] = jnp.zeros((PAD, lanes), jnp.float32)

    for load in loads:
        load.wait()

    outer = (1, rows) if rows > 1 else (1,)
    inner = tuple(range(2, rows))

    for step in range(STEPS):
        now, other = fields[step % 2], fields[(step + 1) % 2]
        last = step == STEPS - 1
        side_each(step, "recv")
        if step > 0:
            side_each(step - 1, "send")

        def advance(y, x):
            middle = now[y, x, inside]
            spread = (
                now[y - 1, x, inside]
                + now[y + 1, x, inside]
                + now[y, x - 1, inside]
                + now[y, x + 1, inside]
                + now[y, x, pl.ds(PAD - 1, depth)]
                + now[y, x, pl.ds(PAD + 1, depth)]
                - 6.0 * middle
            )
            later = 2.0 * middle - other[y, x, inside] + speed[y - 1, x - 1] * spread
            if last:
                end_ref[y - 1, x - 1] = later
            else:
                other[y, x, inside] = later

        @pl.loop(0, chunks)
        def _(chunk):
            def compute(planes):
                if planes:

                    @pl.loop(0, width)
                    def _(offset):
                        for y in planes:
                            advance(y, chunk * width + offset + 1)

            if last:
                compute(inner)
            lat_each(step, chunk, "recv")
            if step > 0:
                lat_each(step - 1, chunk, "send")
            compute(outer)
            if not last:
                compute(inner)
            if not last:
                lat_each(step + 1, chunk, "start")

        if not last:
            side_each(step + 1, "start")

    side_each(STEPS - 1, "send")

    @pl.loop(0, chunks)
    def _(chunk):
        lat_each(STEPS - 1, chunk, "send")


def solution(mesh):
    counts = tuple(mesh.shape[axis] for axis in AXES)

    def shards(pressure, earlier, speed_square):
        rows, columns, depth, lanes = pressure.shape
        chunks = math.gcd(columns, CHUNKS)
        field = pltpu.VMEM((rows + 2, columns + 2, depth + 2 * PAD, lanes), jnp.float32)
        return pl.pallas_call(
            functools.partial(kernel, counts, chunks),
            out_shape=pltpu.VMEM(pressure.shape, jnp.float32),
            in_specs=[pl.BlockSpec(memory_space=pltpu.HBM)] * 3,
            out_specs=pl.BlockSpec(memory_space=pltpu.VMEM),
            scratch_shapes=[
                field,
                field,
                pltpu.VMEM(pressure.shape, jnp.float32),
                pltpu.SemaphoreType.DMA((7,)),
                pltpu.SemaphoreType.DMA((2, 2, chunks)),
                pltpu.SemaphoreType.DMA((2, 2, chunks)),
                pltpu.SemaphoreType.DMA((2, 2, 2)),
                pltpu.SemaphoreType.DMA((2, 2, 2)),
            ],
            compiler_params=pltpu.CompilerParams(
                collective_id=0, has_side_effects=True, vmem_limit_bytes=44 * 2**20
            ),
        )(pressure, earlier, speed_square)

    spec = P("lat", "lon", "lev", None)
    return jax.shard_map(
        shards, mesh=mesh, in_specs=(spec, spec, spec), out_specs=spec, check_vma=False
    )
```

profile of v0, /device:TPU:1, one launch (start us, length us, event | category | flops | bytes accessed | tf_op | source)
XLA Modules:
  0.0 187.8 jit_solution(2024635173975481522)
XLA Ops:
  0.0 184.4 %shard_map.37 = f32[4,64,64,128]{3,2,1,0:T(8,128)S(1)} custom-call(f32[4,64,64,128]{3,2,1,0:T(8,128)} %start_ref.1, f32[4,64,64,128]{3,2,1,0:T(8,128)} %earlier_ref.1, f32[4,64,64,128]{3,2,1,0:T(8,128)} %speed_ref.1), custom_call_target="tpu_custom_call" | custom-call | tf_op jit(solution)/shard_map/pallas_call | solution.py:257
  184.4 3.4 %copy.5 = f32[4,64,64,128]{3,2,1,0:T(8,128)} copy(f32[4,64,64,128]{3,2,1,0:T(8,128)S(1)} %shard_map.37) | data formatting | bytes 16777216
where the time goes:
time: 189 us; the launch traced here: 188 us
  Pallas kernels  184 us (97%)
  local copies, waits for them, and re-layouts  3.4 us (2%)
    pallas_call x1, Pallas kernels, shards(): pl.pallas_call(functools.partial(kernel, counts, chunks), out_shape=pltpu...  184 us

commit v1 on v0

v1 whole, which is shorter than its diff:
```python
import functools

import jax
import jax.numpy as jnp
from jax import lax
from jax.experimental import pallas as pl
from jax.experimental.pallas import tpu as pltpu
from jax.sharding import PartitionSpec as P

STEPS = 4
TAILS = (28, 8)
PAD = 8
AXES = ("lat", "lon", "lev")
MESH = pl.DeviceIdType.MESH


def late():
    return lax.axis_index("lev") % 2 == 0


def neighbours(counts):
    me = [lax.axis_index(axis) for axis in AXES]
    return me, [(place > 0, place < count - 1) for place, count in zip(me, counts)]


def greet(me, has, dims):
    barrier = pltpu.get_barrier_semaphore()
    greeted = jnp.int32(0)
    for dim in dims:
        for side, shift in enumerate((-1, 1)):
            greeted = greeted + has[dim][side].astype(jnp.int32)

            @pl.when(has[dim][side])
            def _():
                pl.semaphore_signal(barrier, inc=1, device_id={AXES[dim]: me[dim] + shift}, device_id_type=MESH)

    pl.semaphore_wait(barrier, greeted)


def each_side(me, has, dim, act, copy_of, also=None):
    incoming = act == "recv"
    for side, shift in enumerate((-1, 1)):
        there = has[dim][1 - side if incoming else side]
        if also is not None:
            there = jnp.logical_and(there, also)

        @pl.when(there)
        def _():
            copy = copy_of(side, me[dim] - shift if incoming else me[dim] + shift)
            if incoming:
                copy.wait_recv()
            elif act == "send":
                copy.wait_send()
            else:
                copy.start()


def main_kernel(
    counts,
    bounds,
    start_ref,
    earlier_ref,
    speed_ref,
    end_ref,
    edge_ref,
    pace_ref,
    even,
    odd,
    speed,
    load_sem,
    lat_send,
    lat_recv,
    side_send,
    side_recv,
):
    rows, columns, depth, lanes = start_ref.shape
    fields = (even, odd)
    inside = pl.ds(PAD, depth)
    me, has = neighbours(counts)
    parts = [(first, after - first) for first, after in zip(bounds, bounds[1:])]
    split, final = bounds[1], len(parts) - 1
    early_first, early_width = parts[final]

    edges = (0, rows - 1)
    early = [
        pltpu.make_async_copy(
            start_ref.at[plane, pl.ds(early_first, early_width)],
            even.at[plane + 1, pl.ds(1 + early_first, early_width), inside],
            load_sem.at[place],
        )
        for place, plane in enumerate(edges)
    ]
    loads = [
        pltpu.make_async_copy(earlier_ref, odd.at[pl.ds(1, rows), pl.ds(1, columns), inside], load_sem.at[2]),
        pltpu.make_async_copy(speed_ref, speed, load_sem.at[3]),
    ] + [
        pltpu.make_async_copy(
            start_ref.at[plane, pl.ds(0, early_first)],
            even.at[plane + 1, pl.ds(1, early_first), inside],
            load_sem.at[4 + place],
        )
        for place, plane in enumerate(edges)
    ]
    loads += [
        pltpu.make_async_copy(
            speed_ref.at[plane, pl.ds(split, columns - split)], pace_ref.at[place], load_sem.at[6 + place]
        )
        for place, plane in enumerate(edges)
    ]
    if rows > 2:
        loads.append(
            pltpu.make_async_copy(
                start_ref.at[pl.ds(1, rows - 2)],
                even.at[pl.ds(2, rows - 2), pl.ds(1, columns), inside],
                load_sem.at[8],
            )
        )
    for load in early:
        load.start()

    greet(me, has, (0, 1, 2))

    def lat_each(step, part, act, held=False):
        field = fields[step % 2]
        first, width = parts[part]

        def copy_of(side, target):
            if step == 0 and not held:
                source = start_ref.at[(0, rows - 1)[side], pl.ds(first, width)]
            else:
                source = field.at[(1, rows)[side], pl.ds(first + 1, width), inside]
            return pltpu.make_async_remote_copy(
                src_ref=source,
                dst_ref=field.at[(rows + 1, 0)[side], pl.ds(first + 1, width), inside],
                send_sem=lat_send.at[side, part],
                recv_sem=lat_recv.at[step % 2, side, part],
                device_id={"lat": target},
                device_id_type=MESH,
            )

        also = late() if step == STEPS - 1 and part > 0 else None
        each_side(me, has, 0, act, copy_of, also)

    def side_each(step, act):
        field = fields[step % 2]
        for dim in (1, 2):

            def copy_of(side, target):
                if dim == 1:
                    if step == 0:
                        source = start_ref.at[:, (0, columns - 1)[side]]
                    else:
                        source = field.at[pl.ds(1, rows), (1, columns)[side], inside]
                    dest = field.at[pl.ds(1, rows), (columns + 1, 0)[side], inside]
                else:
                    if step == 0:
                        source = start_ref.at[:, :, pl.ds((0, depth - PAD)[side], PAD)]
                    else:
                        source = field.at[pl.ds(1, rows), pl.ds(1, columns), pl.ds((PAD, depth)[side], PAD)]
                    dest = field.at[pl.ds(1, rows), pl.ds(1, columns), pl.ds((PAD + depth, 0)[side], PAD)]
                return pltpu.make_async_remote_copy(
                    src_ref=source,
                    dst_ref=dest,
                    send_sem=side_send.at[dim - 1, side],
                    recv_sem=side_recv.at[step % 2, dim - 1, side],
                    device_id={AXES[dim]: target},
                    device_id_type=MESH,
                )

            each_side(me, has, dim, act, copy_of)

    for load in early:
        load.wait()
    lat_each(0, final, "start", held=True)
    for part in range(final):
        lat_each(0, part, "start")
    side_each(0, "start")
    for load in loads:
        load.start()

    for side in (0, 1):

        @pl.when(jnp.logical_not(has[0][side]))
        def _():
            @pl.loop(1, columns + 1)
            def _(x):
                for field in fields:
                    field[(0, rows + 1)[side], x, inside] = jnp.zeros((depth, lanes), jnp.float32)

        @pl.when(jnp.logical_not(has[1][side]))
        def _():
            for field in fields:
                for y in range(1, rows + 1):
                    field[y, (0, columns + 1)[side], inside] = jnp.zeros((depth, lanes), jnp.float32)

        @pl.when(jnp.logical_not(has[2][side]))
        def _():
            @pl.loop(1, columns + 1)
            def _(x):
                for field in fields:
                    for y in range(1, rows + 1):
                        field[y, x, pl.ds((0, PAD + depth)[side], PAD)] = jnp.zeros((PAD, lanes), jnp.float32)

    for load in loads:
        load.wait()

    def advance(step, y, x, low=True, high=True):
        now, other = fields[step % 2], fields[(step + 1) % 2]
        middle = now[y, x, inside]
        spread = now[y, x - 1, inside] + now[y, x + 1, inside]
        if low:
            spread += now[y - 1, x, inside]
        if high:
            spread += now[y + 1, x, inside]
        spread += now[y, x, pl.ds(PAD - 1, depth)] + now[y, x, pl.ds(PAD + 1, depth)] - 6.0 * middle
        return 2.0 * middle - other[y, x, inside] + speed[y - 1, x - 1] * spread

    for step in range(STEPS - 1):
        other = fields[(step + 1) % 2]
        side_each(step, "recv")
        side_each(step, "send")
        for part, (first, width) in enumerate(parts):
            lat_each(step, part, "recv")
            lat_each(step, part, "send", held=part == final)
            keep = step == STEPS - 2 and part > 0

            @pl.loop(first + 1, first + width + 1)
            def _(x):
                for place, y in enumerate((1, rows)):
                    later = advance(step, y, x)
                    other[y, x, inside] = later
                    if keep:
                        edge_ref[place, x - 1 - split] = later

            lat_each(step + 1, part, "start") if part == 0 or step < STEPS - 2 else None
            if step == STEPS - 2 and 0 < part < final:
                lat_each(step + 1, part, "start")

            @pl.loop(first + 1, first + width + 1)
            def _(x):
                for y in range(2, rows):
                    other[y, x, inside] = advance(step, y, x)

        side_each(step + 1, "start")

    step = STEPS - 1
    now = fields[step % 2]
    side_each(step, "recv")

    @pl.loop(1, columns + 1)
    def _(x):
        for y in range(1, rows + 1):
            end_ref[y - 1, x - 1] = advance(step, y, x, low=y > 1, high=y < rows)

    side_each(step, "send")
    for part, (first, width) in enumerate(parts[:-1]):
        lat_each(step, part, "recv")

        def finish():
            @pl.loop(first, first + width)
            def _(x):
                for row, halo in ((0, 0), (rows - 1, rows + 1)):
                    end_ref[row, x] = end_ref[row, x] + speed[row, x] * now[halo, x + 1, inside]

        finish() if part == 0 else pl.when(late())(finish)
        lat_each(step, part, "send")


def tail_kernel(counts, bounds, end_ref, edge_ref, pace_ref, token_ref, last_ref, halo, send, recv):
    rows = end_ref.shape[0]
    split, columns = bounds[1], bounds[-1]
    me, has = neighbours(counts)
    greet(me, has, (0,))
    parts = list(enumerate(zip(bounds[1:], bounds[2:])))

    def lat_each(part, first, after, act):
        span = pl.ds(first - split, after - first)

        def copy_of(side, target):
            return pltpu.make_async_remote_copy(
                src_ref=edge_ref.at[side, span],
                dst_ref=halo.at[1 - side, span],
                send_sem=send.at[side, part],
                recv_sem=recv.at[side, part],
                device_id={"lat": target},
                device_id_type=MESH,
            )

        each_side(me, has, 0, act, copy_of, None if part == len(parts) - 1 else jnp.logical_not(late()))

    for part, (first, after) in parts:
        lat_each(part, first, after, "start")
    for part, (first, after) in parts:
        lat_each(part, first, after, "recv")

        def finish():
            for place, row in enumerate((0, rows - 1)):

                @pl.when(has[0][place])
                def _():
                    @pl.loop(first, after)
                    def _(x):
                        last_ref[place, x - split] = end_ref[row, x] + pace_ref[place, x - split] * halo[place, x - split]

                @pl.when(jnp.logical_not(has[0][place]))
                def _():
                    @pl.loop(first, after)
                    def _(x):
                        last_ref[place, x - split] = end_ref[row, x]

        finish() if part == len(parts) - 1 else pl.when(jnp.logical_not(late()))(finish)
    for part, (first, after) in parts:
        lat_each(part, first, after, "send")


def run(copies, there=None):
    def go():
        for copy in copies:
            copy.start()
        for copy in copies:
            copy.wait()

    go() if there is None else pl.when(there)(go)


def write_kernel(bounds, end_ref, out_ref, token_ref, sem):
    token_ref[...] = jnp.zeros_like(token_ref)
    rows, columns = out_ref.shape[:2]
    split, after = bounds[1], bounds[2]
    pieces = [(0, pl.ds(0, split)), (rows - 1, pl.ds(0, split))] + [(row, pl.ds(0, columns)) for row in range(1, rows - 1)]
    more = [(0, pl.ds(split, after - split)), (rows - 1, pl.ds(split, after - split))]
    copies = [
        pltpu.make_async_copy(end_ref.at[row, span], out_ref.at[row, span], sem.at[place])
        for place, (row, span) in enumerate(pieces + more)
    ]
    lagging = copies[len(pieces) :]

    @pl.when(late())
    def _():
        for copy in lagging:
            copy.start()

    run(copies[: len(pieces)])

    @pl.when(late())
    def _():
        for copy in lagging:
            copy.wait()


def patch_kernel(bounds, whole_ref, last_ref, out_ref, sem):
    rows, columns = out_ref.shape[:2]
    split = bounds[1]
    for first, there in ((split, jnp.logical_not(late())), (bounds[2], late())):
        run(
            [
                pltpu.make_async_copy(
                    last_ref.at[place, pl.ds(first - split, columns - first)],
                    out_ref.at[row, pl.ds(first, columns - first)],
                    sem.at[place],
                )
                for place, row in enumerate((0, rows - 1))
            ],
            there,
        )


def solution(mesh):
    counts = tuple(mesh.shape[axis] for axis in AXES)
    vmem, hbm = pl.BlockSpec(memory_space=pltpu.VMEM), pl.BlockSpec(memory_space=pltpu.HBM)
    dma = pltpu.SemaphoreType.DMA

    def shards(pressure, earlier, speed_square):
        rows, columns, depth, lanes = pressure.shape
        bounds = (0,) + tuple(columns - columns * tail // 64 for tail in TAILS) + (columns,)
        parts = len(bounds) - 1
        edge = (2, columns - bounds[1], depth, lanes)
        field = pltpu.VMEM((rows + 2, columns + 2, depth + 2 * PAD, lanes), jnp.float32)
        end, edges, paces = pl.pallas_call(
            functools.partial(main_kernel, counts, bounds),
            out_shape=(pltpu.VMEM(pressure.shape, jnp.float32), pltpu.VMEM(edge, jnp.float32), pltpu.VMEM(edge, jnp.float32)),
            in_specs=[hbm] * 3,
            out_specs=(vmem,) * 3,
            scratch_shapes=[
                field,
                field,
                pltpu.VMEM(pressure.shape, jnp.float32),
                dma((9,)),
                dma((2, parts)),
                dma((2, 2, parts)),
                dma((2, 2)),
                dma((2, 2, 2)),
            ],
            compiler_params=pltpu.CompilerParams(
                collective_id=0, has_side_effects=True, vmem_limit_bytes=44 * 2**20
            ),
        )(pressure, earlier, speed_square)
        out, token = pl.pallas_call(
            functools.partial(write_kernel, bounds),
            out_shape=(pltpu.HBM(pressure.shape, jnp.float32), pltpu.VMEM((8, 128), jnp.float32)),
            in_specs=[vmem],
            out_specs=(hbm, vmem),
            scratch_shapes=[dma((rows + 2,))],
            compiler_params=pltpu.CompilerParams(vmem_limit_bytes=2**20),
        )(end)
        last = pl.pallas_call(
            functools.partial(tail_kernel, counts, bounds),
            out_shape=pltpu.VMEM(edge, jnp.float32),
            in_specs=[vmem] * 4,
            out_specs=vmem,
            scratch_shapes=[
                pltpu.VMEM(edge, jnp.float32),
                dma((2, parts - 1)),
                dma((2, parts - 1)),
            ],
            compiler_params=pltpu.CompilerParams(
                collective_id=1, has_side_effects=True, vmem_limit_bytes=4 * 2**20
            ),
        )(end, edges, paces, token)
        return pl.pallas_call(
            functools.partial(patch_kernel, bounds),
            out_shape=pltpu.HBM(pressure.shape, jnp.float32),
            in_specs=[hbm, vmem],
            out_specs=hbm,
            input_output_aliases={0: 0},
            scratch_shapes=[dma((2,))],
            compiler_params=pltpu.CompilerParams(vmem_limit_bytes=2**20),
        )(out, last)

    spec = P("lat", "lon", "lev", None)
    return jax.shard_map(shards, mesh=mesh, in_specs=(spec, spec, spec), out_specs=spec, check_vma=False)
```

time: 189 us -> 186 us (0.984); the launches traced: 188 us -> 183 us
  local copies, waits for them, and re-layouts: 3.4 us -> 0 us
    unnamed x1 -> x0, local copies, waits for them, and re-layouts: 3.4 us -> none
    pallas_call x1 -> x4, Pallas kernels: 184 us -> 183 us  [the longest x1 164 us: shards(): pl.pallas_call(functools.partial(main_kernel, counts, bounds), out_shape=...]
where the time goes in v1:
time: 186 us; the launch traced here: 183 us
  Pallas kernels  183 us (98%)
    pallas_call x1, Pallas kernels, shards(): pl.pallas_call(functools.partial(main_kernel, counts, bounds), out_shape=...  164 us
    pallas_call x1, Pallas kernels, shards(): pl.pallas_call(functools.partial(tail_kernel, counts, bounds), out_shape=...  14.2 us

profile of v1, /device:TPU:1, one launch (start us, length us, event | category | flops | bytes accessed | tf_op | source)
XLA Modules:
  0.0 182.8 jit_solution(17245233224802122784)
XLA Ops:
  0.0 164.5 %shard_map.37 = (f32[4,64,64,128]{3,2,1,0:T(8,128)S(1)}, f32[2,28,64,128]{3,2,1,0:T(8,128)S(1)}, f32[2,28,64,128]{3,2,1,0:T(8,128)S(1)}) custom-call(f32[4,64,64,128]{3,2,1,0:T(8,128)} %start_ref.1, f32[4,64,64,128]{3,2,1,0:T(8,128)} %earlier_ref.1, f32[4,64,64,128]{3,2,1,0:T(8,128)} %speed_ref.1), custom_call_target="tpu_custom_call" | custom-call | tf_op jit(solution)/shard_map/pallas_call | solution.py:379
  164.5 2.9 %shard_map.38 = (f32[4,64,64,128]{3,2,1,0:T(8,128)}, f32[8,128]{1,0:T(8,128)S(1)}) custom-call(f32[4,64,64,128]{3,2,1,0:T(8,128)S(1)} %get-tuple-element.10.end_ref), custom_call_target="tpu_custom_call" | custom-call | tf_op jit(solution)/shard_map/pallas_call | solution.py:398
  167.3 14.2 %shard_map.39.last_ref = f32[2,28,64,128]{3,2,1,0:T(8,128)S(1)} custom-call(f32[4,64,64,128]{3,2,1,0:T(8,128)S(1)} %get-tuple-element.10.end_ref, f32[2,28,64,128]{3,2,1,0:T(8,128)S(1)} %get-tuple-element.12.edge_ref, f32[2,28,64,128]{3,2,1,0:T(8,128)S(1)} %get-tuple-element.13.pace_ref, f32[8,128]{1,0:T(8,128)S(1)} %get-tuple-element.14.token_ref), custom_call_target="tpu_custom_call" | custom-call | tf_op jit(solution)/shard_map/pallas_call | solution.py:406
  181.5 1.3 shard_map.40

commit v2 on v1

--- a/solution.py
+++ b/solution.py
@@ -8,7 +8,7 @@
 from jax.sharding import PartitionSpec as P
 
 STEPS = 4
-TAILS = (28, 8)
+TAILS = (24, 8)
 PAD = 8
 AXES = ("lat", "lon", "lev")
 MESH = pl.DeviceIdType.MESH
@@ -37,9 +37,10 @@
     pl.semaphore_wait(barrier, greeted)
 
 
-def each_side(me, has, dim, act, copy_of, also=None):
+def each_side(me, has, dim, act, copy_of, also=None, sides=(0, 1)):
     incoming = act == "recv"
-    for side, shift in enumerate((-1, 1)):
+    for side in sides:
+        shift = (-1, 1)[side]
         there = has[dim][1 - side if incoming else side]
         if also is not None:
             there = jnp.logical_and(there, also)
@@ -72,6 +73,9 @@
     lat_recv,
     side_send,
     side_recv,
+    reply_sem,
+    level_sem,
+    beside_sem,
 ):
     rows, columns, depth, lanes = start_ref.shape
     fields = (even, odd)
@@ -118,9 +122,28 @@
     for load in early:
         load.start()
 
-    greet(me, has, (0, 1, 2))
-
-    def lat_each(step, part, act, held=False):
+    low, high = has[0]
+    bottom = jnp.logical_not(low)
+    barrier = pltpu.get_barrier_semaphore()
+    beside = sum(there.astype(jnp.int32) for dim in (1, 2) for there in has[dim])
+
+    def tell_beside(sem):
+        for dim in (1, 2):
+            for side, shift in enumerate((-1, 1)):
+
+                @pl.when(has[dim][side])
+                def _():
+                    pl.semaphore_signal(sem, inc=1, device_id={AXES[dim]: me[dim] + shift}, device_id_type=MESH)
+
+    @pl.when(high)
+    def _():
+        pl.semaphore_signal(barrier, inc=1, device_id={"lat": me[0] + 1}, device_id_type=MESH)
+
+    @pl.when(bottom)
+    def _():
+        tell_beside(barrier)
+
+    def lat_each(step, part, act, held=False, sides=(0, 1)):
         field = fields[step % 2]
         first, width = parts[part]
 
@@ -139,7 +162,7 @@
             )
 
         also = late() if step == STEPS - 1 and part > 0 else None
-        each_side(me, has, 0, act, copy_of, also)
+        each_side(me, has, 0, act, copy_of, also, sides)
 
     def side_each(step, act):
         field = fields[step % 2]
@@ -171,12 +194,42 @@
 
     for load in early:
         load.wait()
-    lat_each(0, final, "start", held=True)
-    for part in range(final):
-        lat_each(0, part, "start")
-    side_each(0, "start")
+
+    def lat_first(side):
+        lat_each(0, final, "start", held=True, sides=(side,))
+        for part in range(final):
+            lat_each(0, part, "start", sides=(side,))
+
+    @pl.when(low)
+    def _():
+        pl.semaphore_wait(barrier, 1)
+        pl.semaphore_signal(reply_sem, inc=1, device_id={"lat": me[0] - 1}, device_id_type=MESH)
+
+    lat_first(0)
+
+    @pl.when(high)
+    def _():
+        pl.semaphore_wait(reply_sem, 1)
+
+    lat_first(1)
     for load in loads:
         load.start()
+
+    @pl.when(bottom)
+    def _():
+        pl.semaphore_wait(barrier, beside)
+
+    @pl.when(low)
+    def _():
+        pl.semaphore_wait(level_sem, 1)
+
+    @pl.when(high)
+    def _():
+        tell_beside(beside_sem)
+        pl.semaphore_wait(beside_sem, beside)
+        pl.semaphore_signal(level_sem, inc=1, device_id={"lat": me[0] + 1}, device_id_type=MESH)
+
+    side_each(0, "start")
 
     for side in (0, 1):
 
@@ -232,9 +285,7 @@
                     if keep:
                         edge_ref[place, x - 1 - split] = later
 
-            lat_each(step + 1, part, "start") if part == 0 or step < STEPS - 2 else None
-            if step == STEPS - 2 and 0 < part < final:
-                lat_each(step + 1, part, "start")
+            lat_each(step + 1, part, "start")
 
             @pl.loop(first + 1, first + width + 1)
             def _(x):
@@ -253,7 +304,7 @@
             end_ref[y - 1, x - 1] = advance(step, y, x, low=y > 1, high=y < rows)
 
     side_each(step, "send")
-    for part, (first, width) in enumerate(parts[:-1]):
+    for part, (first, width) in enumerate(parts):
         lat_each(step, part, "recv")
 
         def finish():
@@ -270,7 +321,12 @@
     rows = end_ref.shape[0]
     split, columns = bounds[1], bounds[-1]
     me, has = neighbours(counts)
-    greet(me, has, (0,))
+    mine = jnp.logical_not(late())
+
+    @pl.when(mine)
+    def _():
+        greet(me, has, (0,))
+
     parts = list(enumerate(zip(bounds[1:], bounds[2:])))
 
     def lat_each(part, first, after, act):
@@ -286,7 +342,7 @@
                 device_id_type=MESH,
             )
 
-        each_side(me, has, 0, act, copy_of, None if part == len(parts) - 1 else jnp.logical_not(late()))
+        each_side(me, has, 0, act, copy_of, mine)
 
     for part, (first, after) in parts:
         lat_each(part, first, after, "start")
@@ -308,7 +364,7 @@
                     def _(x):
                         last_ref[place, x - split] = end_ref[row, x]
 
-        finish() if part == len(parts) - 1 else pl.when(jnp.logical_not(late()))(finish)
+        pl.when(mine)(finish)
     for part, (first, after) in parts:
         lat_each(part, first, after, "send")
 
@@ -326,9 +382,9 @@
 def write_kernel(bounds, end_ref, out_ref, token_ref, sem):
     token_ref[...] = jnp.zeros_like(token_ref)
     rows, columns = out_ref.shape[:2]
-    split, after = bounds[1], bounds[2]
+    split = bounds[1]
     pieces = [(0, pl.ds(0, split)), (rows - 1, pl.ds(0, split))] + [(row, pl.ds(0, columns)) for row in range(1, rows - 1)]
-    more = [(0, pl.ds(split, after - split)), (rows - 1, pl.ds(split, after - split))]
+    more = [(0, pl.ds(split, columns - split)), (rows - 1, pl.ds(split, columns - split))]
     copies = [
         pltpu.make_async_copy(end_ref.at[row, span], out_ref.at[row, span], sem.at[place])
         for place, (row, span) in enumerate(pieces + more)
@@ -350,19 +406,14 @@
 
 def patch_kernel(bounds, whole_ref, last_ref, out_ref, sem):
     rows, columns = out_ref.shape[:2]
-    split = bounds[1]
-    for first, there in ((split, jnp.logical_not(late())), (bounds[2], late())):
-        run(
-            [
-                pltpu.make_async_copy(
-                    last_ref.at[place, pl.ds(first - split, columns - first)],
-                    out_ref.at[row, pl.ds(first, columns - first)],
-                    sem.at[place],
-                )
-                for place, row in enumerate((0, rows - 1))
-            ],
-            there,
-        )
+    span = pl.ds(bounds[1], columns - bounds[1])
+    run(
+        [
+            pltpu.make_async_copy(last_ref.at[place], out_ref.at[row, span], sem.at[place])
+            for place, row in enumerate((0, rows - 1))
+        ],
+        jnp.logical_not(late()),
+    )
 
 
 def solution(mesh):
@@ -390,7 +441,8 @@
                 dma((2, 2, parts)),
                 dma((2, 2)),
                 dma((2, 2, 2)),
-            ],
+            ]
+            + [pltpu.SemaphoreType.REGULAR] * 3,
             compiler_params=pltpu.CompilerParams(
                 collective_id=0, has_side_effects=True, vmem_limit_bytes=44 * 2**20
             ),

time: 186 us -> 185 us (level); the launches traced: 183 us -> 185 us
  Pallas kernels: 183 us -> 185 us
    pallas_call x1, Pallas kernels: 164 us -> 167 us  [shards(): pl.pallas_call(functools.partial(main_kernel, counts, bounds), out_shape=...]
where the time goes in v2:
time: 185 us
  Pallas kernels  185 us (100%)
    pallas_call x1, Pallas kernels, shards(): pl.pallas_call(functools.partial(main_kernel, counts, bounds), out_shape=...  167 us
    pallas_call x1, Pallas kernels, shards(): pl.pallas_call(functools.partial(tail_kernel, counts, bounds), out_shape=...  13.7 us

profile of v2, /device:TPU:1, one launch (start us, length us, event | category | flops | bytes accessed | tf_op | source)
XLA Modules:
  0.0 185.2 jit_solution(6572492656872346785)
XLA Ops:
  0.0 167.4 %shard_map.37 = (f32[4,64,64,128]{3,2,1,0:T(8,128)S(1)}, f32[2,24,64,128]{3,2,1,0:T(8,128)S(1)}, f32[2,24,64,128]{3,2,1,0:T(8,128)S(1)}) custom-call(f32[4,64,64,128]{3,2,1,0:T(8,128)} %start_ref.1, f32[4,64,64,128]{3,2,1,0:T(8,128)} %earlier_ref.1, f32[4,64,64,128]{3,2,1,0:T(8,128)} %speed_ref.1), custom_call_target="tpu_custom_call" | custom-call | tf_op jit(solution)/shard_map/pallas_call | solution.py:430
  167.4 2.9 %shard_map.38 = (f32[4,64,64,128]{3,2,1,0:T(8,128)}, f32[8,128]{1,0:T(8,128)S(1)}) custom-call(f32[4,64,64,128]{3,2,1,0:T(8,128)S(1)} %get-tuple-element.10.end_ref), custom_call_target="tpu_custom_call" | custom-call | tf_op jit(solution)/shard_map/pallas_call | solution.py:450
  170.3 13.7 %shard_map.39.last_ref = f32[2,24,64,128]{3,2,1,0:T(8,128)S(1)} custom-call(f32[4,64,64,128]{3,2,1,0:T(8,128)S(1)} %get-tuple-element.10.end_ref, f32[2,24,64,128]{3,2,1,0:T(8,128)S(1)} %get-tuple-element.12.edge_ref, f32[2,24,64,128]{3,2,1,0:T(8,128)S(1)} %get-tuple-element.13.pace_ref, f32[8,128]{1,0:T(8,128)S(1)} %get-tuple-element.14.token_ref), custom_call_target="tpu_custom_call" | custom-call | tf_op jit(solution)/shard_map/pallas_call | solution.py:458
  184.0 1.2 shard_map.40

commit v3 on v2

--- a/solution.py
+++ b/solution.py
@@ -8,7 +8,9 @@
 from jax.sharding import PartitionSpec as P
 
 STEPS = 4
-TAILS = (24, 8)
+TAIL = 20
+EARLY = 4
+END = 2
 PAD = 8
 AXES = ("lat", "lon", "lev")
 MESH = pl.DeviceIdType.MESH
@@ -59,6 +61,7 @@
 def main_kernel(
     counts,
     bounds,
+    early_first,
     start_ref,
     earlier_ref,
     speed_ref,
@@ -82,45 +85,45 @@
     inside = pl.ds(PAD, depth)
     me, has = neighbours(counts)
     parts = [(first, after - first) for first, after in zip(bounds, bounds[1:])]
-    split, final = bounds[1], len(parts) - 1
-    early_first, early_width = parts[final]
-
-    edges = (0, rows - 1)
+    split = bounds[1]
+
     early = [
         pltpu.make_async_copy(
-            start_ref.at[plane, pl.ds(early_first, early_width)],
-            even.at[plane + 1, pl.ds(1 + early_first, early_width), inside],
+            start_ref.at[plane, pl.ds(early_first, columns - early_first)],
+            even.at[plane + 1, pl.ds(1 + early_first, columns - early_first), inside],
             load_sem.at[place],
         )
-        for place, plane in enumerate(edges)
+        for place, plane in enumerate((0, rows - 1))
     ]
-    loads = [
-        pltpu.make_async_copy(earlier_ref, odd.at[pl.ds(1, rows), pl.ds(1, columns), inside], load_sem.at[2]),
-        pltpu.make_async_copy(speed_ref, speed, load_sem.at[3]),
-    ] + [
+    starts = [
         pltpu.make_async_copy(
-            start_ref.at[plane, pl.ds(0, early_first)],
-            even.at[plane + 1, pl.ds(1, early_first), inside],
-            load_sem.at[4 + place],
+            start_ref.at[:, pl.ds(0, early_first)],
+            even.at[pl.ds(1, rows), pl.ds(1, early_first), inside],
+            load_sem.at[2],
         )
-        for place, plane in enumerate(edges)
-    ]
-    loads += [
-        pltpu.make_async_copy(
-            speed_ref.at[plane, pl.ds(split, columns - split)], pace_ref.at[place], load_sem.at[6 + place]
-        )
-        for place, plane in enumerate(edges)
     ]
     if rows > 2:
-        loads.append(
+        starts.append(
             pltpu.make_async_copy(
-                start_ref.at[pl.ds(1, rows - 2)],
-                even.at[pl.ds(2, rows - 2), pl.ds(1, columns), inside],
-                load_sem.at[8],
+                start_ref.at[pl.ds(1, rows - 2), pl.ds(early_first, columns - early_first)],
+                even.at[pl.ds(2, rows - 2), pl.ds(1 + early_first, columns - early_first), inside],
+                load_sem.at[3],
             )
         )
+    loads = [
+        pltpu.make_async_copy(earlier_ref, odd.at[pl.ds(1, rows), pl.ds(1, columns), inside], load_sem.at[4]),
+        pltpu.make_async_copy(speed_ref, speed, load_sem.at[5]),
+    ]
+    behind = late()
+    ahead = jnp.logical_not(behind)
+
     for load in early:
         load.start()
+
+    @pl.when(behind)
+    def _():
+        for load in starts:
+            load.start()
 
     low, high = has[0]
     bottom = jnp.logical_not(low)
@@ -143,15 +146,19 @@
     def _():
         tell_beside(barrier)
 
-    def lat_each(step, part, act, held=False, sides=(0, 1)):
+    @pl.when(low)
+    def _():
+        pl.semaphore_wait(barrier, 1)
+        pl.semaphore_signal(reply_sem, inc=1, device_id={"lat": me[0] - 1}, device_id_type=MESH)
+
+    def lat_piece(step, part, act, first, width, also=None, sides=(0, 1), held=True):
         field = fields[step % 2]
-        first, width = parts[part]
 
         def copy_of(side, target):
-            if step == 0 and not held:
+            if held:
+                source = field.at[(1, rows)[side], pl.ds(first + 1, width), inside]
+            else:
                 source = start_ref.at[(0, rows - 1)[side], pl.ds(first, width)]
-            else:
-                source = field.at[(1, rows)[side], pl.ds(first + 1, width), inside]
             return pltpu.make_async_remote_copy(
                 src_ref=source,
                 dst_ref=field.at[(rows + 1, 0)[side], pl.ds(first + 1, width), inside],
@@ -161,8 +168,17 @@
                 device_id_type=MESH,
             )
 
-        also = late() if step == STEPS - 1 and part > 0 else None
         each_side(me, has, 0, act, copy_of, also, sides)
+
+    def lat_each(step, part, act):
+        lat_piece(step, part, act, *parts[part], behind if step == STEPS - 1 and part > 0 else None)
+
+    def lat_first(side):
+        lat_piece(0, 1, "start", early_first, columns - early_first, ahead, (side,))
+        lat_piece(0, 0, "start", 0, split, ahead, (side,), held=False)
+        lat_piece(0, 1, "start", split, early_first - split, ahead, (side,), held=False)
+        for part, piece in enumerate(parts):
+            lat_piece(0, part, "start", *piece, behind, (side,))
 
     def side_each(step, act):
         field = fields[step % 2]
@@ -195,15 +211,10 @@
     for load in early:
         load.wait()
 
-    def lat_first(side):
-        lat_each(0, final, "start", held=True, sides=(side,))
-        for part in range(final):
-            lat_each(0, part, "start", sides=(side,))
-
-    @pl.when(low)
-    def _():
-        pl.semaphore_wait(barrier, 1)
-        pl.semaphore_signal(reply_sem, inc=1, device_id={"lat": me[0] - 1}, device_id_type=MESH)
+    @pl.when(behind)
+    def _():
+        for load in starts:
+            load.wait()
 
     lat_first(0)
 
@@ -212,6 +223,12 @@
         pl.semaphore_wait(reply_sem, 1)
 
     lat_first(1)
+
+    @pl.when(ahead)
+    def _():
+        for load in starts:
+            load.start()
+
     for load in loads:
         load.start()
 
@@ -253,6 +270,11 @@
                 for field in fields:
                     for y in range(1, rows + 1):
                         field[y, x, pl.ds((0, PAD + depth)[side], PAD)] = jnp.zeros((PAD, lanes), jnp.float32)
+
+    @pl.when(ahead)
+    def _():
+        for load in starts:
+            load.wait()
 
     for load in loads:
         load.wait()
@@ -274,7 +296,7 @@
         side_each(step, "send")
         for part, (first, width) in enumerate(parts):
             lat_each(step, part, "recv")
-            lat_each(step, part, "send", held=part == final)
+            lat_each(step, part, "send")
             keep = step == STEPS - 2 and part > 0
 
             @pl.loop(first + 1, first + width + 1)
@@ -284,6 +306,7 @@
                     other[y, x, inside] = later
                     if keep:
                         edge_ref[place, x - 1 - split] = later
+                        pace_ref[place, x - 1 - split] = speed[y - 1, x - 1]
 
             lat_each(step + 1, part, "start")
 
@@ -313,60 +336,54 @@
                 for row, halo in ((0, 0), (rows - 1, rows + 1)):
                     end_ref[row, x] = end_ref[row, x] + speed[row, x] * now[halo, x + 1, inside]
 
-        finish() if part == 0 else pl.when(late())(finish)
+        finish() if part == 0 else pl.when(behind)(finish)
         lat_each(step, part, "send")
 
 
-def tail_kernel(counts, bounds, end_ref, edge_ref, pace_ref, token_ref, last_ref, halo, send, recv):
-    rows = end_ref.shape[0]
-    split, columns = bounds[1], bounds[-1]
+def tail_kernel(counts, pieces, end_ref, edge_ref, pace_ref, token_ref, last_ref, halo, send, recv):
+    rows, columns = end_ref.shape[:2]
+    width = edge_ref.shape[1]
     me, has = neighbours(counts)
-    mine = jnp.logical_not(late())
-
-    @pl.when(mine)
-    def _():
-        greet(me, has, (0,))
-
-    parts = list(enumerate(zip(bounds[1:], bounds[2:])))
-
-    def lat_each(part, first, after, act):
-        span = pl.ds(first - split, after - first)
+
+    def lat_each(piece, act):
+        span = pl.ds(pieces[piece], pieces[piece + 1] - pieces[piece])
 
         def copy_of(side, target):
             return pltpu.make_async_remote_copy(
                 src_ref=edge_ref.at[side, span],
                 dst_ref=halo.at[1 - side, span],
-                send_sem=send.at[side, part],
-                recv_sem=recv.at[side, part],
+                send_sem=send.at[side, piece],
+                recv_sem=recv.at[side, piece],
                 device_id={"lat": target},
                 device_id_type=MESH,
             )
 
-        each_side(me, has, 0, act, copy_of, mine)
-
-    for part, (first, after) in parts:
-        lat_each(part, first, after, "start")
-    for part, (first, after) in parts:
-        lat_each(part, first, after, "recv")
-
-        def finish():
+        each_side(me, has, 0, act, copy_of)
+
+    @pl.when(jnp.logical_not(late()))
+    def _():
+        greet(me, has, (0,))
+        every = range(len(pieces) - 1)
+        for piece in every:
+            lat_each(piece, "start")
+        for piece in every:
+            lat_each(piece, "recv")
             for place, row in enumerate((0, rows - 1)):
 
                 @pl.when(has[0][place])
                 def _():
-                    @pl.loop(first, after)
+                    @pl.loop(pieces[piece], pieces[piece + 1])
                     def _(x):
-                        last_ref[place, x - split] = end_ref[row, x] + pace_ref[place, x - split] * halo[place, x - split]
+                        last_ref[place, x] = end_ref[row, columns - width + x] + pace_ref[place, x] * halo[place, x]
 
                 @pl.when(jnp.logical_not(has[0][place]))
                 def _():
-                    @pl.loop(first, after)
+                    @pl.loop(pieces[piece], pieces[piece + 1])
                     def _(x):
-                        last_ref[place, x - split] = end_ref[row, x]
-
-        pl.when(mine)(finish)
-    for part, (first, after) in parts:
-        lat_each(part, first, after, "send")
+                        last_ref[place, x] = end_ref[row, columns - width + x]
+
+        for piece in every:
+            lat_each(piece, "send")
 
 
 def run(copies, there=None):
@@ -423,12 +440,14 @@
 
     def shards(pressure, earlier, speed_square):
         rows, columns, depth, lanes = pressure.shape
-        bounds = (0,) + tuple(columns - columns * tail // 64 for tail in TAILS) + (columns,)
+        bounds = (0, columns - columns * TAIL // 64, columns)
+        pieces = (0, bounds[2] - bounds[1] - columns * END // 64, bounds[2] - bounds[1])
+        early_first = columns - columns * EARLY // 64
         parts = len(bounds) - 1
         edge = (2, columns - bounds[1], depth, lanes)
         field = pltpu.VMEM((rows + 2, columns + 2, depth + 2 * PAD, lanes), jnp.float32)
         end, edges, paces = pl.pallas_call(
-            functools.partial(main_kernel, counts, bounds),
+            functools.partial(main_kernel, counts, bounds, early_first),
             out_shape=(pltpu.VMEM(pressure.shape, jnp.float32), pltpu.VMEM(edge, jnp.float32), pltpu.VMEM(edge, jnp.float32)),
             in_specs=[hbm] * 3,
             out_specs=(vmem,) * 3,
@@ -436,7 +455,7 @@
                 field,
                 field,
                 pltpu.VMEM(pressure.shape, jnp.float32),
-                dma((9,)),
+                dma((6,)),
                 dma((2, parts)),
                 dma((2, 2, parts)),
                 dma((2, 2)),
@@ -456,14 +475,14 @@
             compiler_params=pltpu.CompilerParams(vmem_limit_bytes=2**20),
         )(end)
         last = pl.pallas_call(
-            functools.partial(tail_kernel, counts, bounds),
+            functools.partial(tail_kernel, counts, pieces),
             out_shape=pltpu.VMEM(edge, jnp.float32),
             in_specs=[vmem] * 4,
             out_specs=vmem,
             scratch_shapes=[
                 pltpu.VMEM(edge, jnp.float32),
-                dma((2, parts - 1)),
-                dma((2, parts - 1)),
+                dma((2, 2)),
+                dma((2, 2)),
             ],
             compiler_params=pltpu.CompilerParams(
                 collective_id=1, has_side_effects=True, vmem_limit_bytes=4 * 2**20

time: 185 us -> 185 us (level)
  no operation moved by 1% of the time
where the time goes in v3:
time: 185 us
  Pallas kernels  185 us (100%)
    pallas_call x1, Pallas kernels, shards(): pl.pallas_call(functools.partial(main_kernel, counts, bounds, early_first...  168 us
    pallas_call x1, Pallas kernels, shards(): pl.pallas_call(functools.partial(tail_kernel, counts, pieces), out_shape=...  13.2 us

profile of v3, /device:TPU:1, one launch (start us, length us, event | category | flops | bytes accessed | tf_op | source)
XLA Modules:
  0.0 185.0 jit_solution(8074054232149583739)
XLA Ops:
  0.0 167.7 %shard_map.37 = (f32[4,64,64,128]{3,2,1,0:T(8,128)S(1)}, f32[2,20,64,128]{3,2,1,0:T(8,128)S(1)}, f32[2,20,64,128]{3,2,1,0:T(8,128)S(1)}) custom-call(f32[4,64,64,128]{3,2,1,0:T(8,128)} %start_ref.1, f32[4,64,64,128]{3,2,1,0:T(8,128)} %earlier_ref.1, f32[4,64,64,128]{3,2,1,0:T(8,128)} %speed_ref.1), custom_call_target="tpu_custom_call" | custom-call | tf_op jit(solution)/shard_map/pallas_call | solution.py:449
  167.7 3.0 %shard_map.38 = (f32[4,64,64,128]{3,2,1,0:T(8,128)}, f32[8,128]{1,0:T(8,128)S(1)}) custom-call(f32[4,64,64,128]{3,2,1,0:T(8,128)S(1)} %get-tuple-element.10.end_ref), custom_call_target="tpu_custom_call" | custom-call | tf_op jit(solution)/shard_map/pallas_call | solution.py:469
  170.7 13.2 %shard_map.39.last_ref = f32[2,20,64,128]{3,2,1,0:T(8,128)S(1)} custom-call(f32[4,64,64,128]{3,2,1,0:T(8,128)S(1)} %get-tuple-element.10.end_ref, f32[2,20,64,128]{3,2,1,0:T(8,128)S(1)} %get-tuple-element.12.edge_ref, f32[2,20,64,128]{3,2,1,0:T(8,128)S(1)} %get-tuple-element.13.pace_ref, f32[8,128]{1,0:T(8,128)S(1)} %get-tuple-element.14.token_ref), custom_call_target="tpu_custom_call" | custom-call | tf_op jit(solution)/shard_map/pallas_call | solution.py:477
  183.9 1.1 shard_map.40

commit v4 on v3

--- a/solution.py
+++ b/solution.py
@@ -376,60 +376,45 @@
                     def _(x):
                         last_ref[place, x] = end_ref[row, columns - width + x] + pace_ref[place, x] * halo[place, x]
 
-                @pl.when(jnp.logical_not(has[0][place]))
-                def _():
-                    @pl.loop(pieces[piece], pieces[piece + 1])
-                    def _(x):
-                        last_ref[place, x] = end_ref[row, columns - width + x]
-
         for piece in every:
             lat_each(piece, "send")
 
 
-def run(copies, there=None):
-    def go():
-        for copy in copies:
-            copy.start()
-        for copy in copies:
-            copy.wait()
-
-    go() if there is None else pl.when(there)(go)
-
-
-def write_kernel(bounds, end_ref, out_ref, token_ref, sem):
+def run(copies):
+    for act in ("start", "wait"):
+        for copy, there in copies:
+            pl.when(there)(getattr(copy, act))
+
+
+def write_kernel(counts, bounds, end_ref, out_ref, token_ref, sem):
     token_ref[...] = jnp.zeros_like(token_ref)
     rows, columns = out_ref.shape[:2]
     split = bounds[1]
-    pieces = [(0, pl.ds(0, split)), (rows - 1, pl.ds(0, split))] + [(row, pl.ds(0, columns)) for row in range(1, rows - 1)]
-    more = [(0, pl.ds(split, columns - split)), (rows - 1, pl.ds(split, columns - split))]
-    copies = [
-        pltpu.make_async_copy(end_ref.at[row, span], out_ref.at[row, span], sem.at[place])
-        for place, (row, span) in enumerate(pieces + more)
-    ]
-    lagging = copies[len(pieces) :]
-
-    @pl.when(late())
-    def _():
-        for copy in lagging:
-            copy.start()
-
-    run(copies[: len(pieces)])
-
-    @pl.when(late())
-    def _():
-        for copy in lagging:
-            copy.wait()
-
-
-def patch_kernel(bounds, whole_ref, last_ref, out_ref, sem):
+    _, has = neighbours(counts)
+    pieces = [(row, pl.ds(0, columns), True) for row in range(1, rows - 1)]
+    for place, row in enumerate((0, rows - 1)):
+        final = jnp.logical_or(late(), jnp.logical_not(has[0][place]))
+        pieces += [(row, pl.ds(0, split), True), (row, pl.ds(split, columns - split), final)]
+    run(
+        [
+            (pltpu.make_async_copy(end_ref.at[row, span], out_ref.at[row, span], sem.at[place]), there)
+            for place, (row, span, there) in enumerate(pieces)
+        ]
+    )
+
+
+def patch_kernel(counts, bounds, whole_ref, last_ref, out_ref, sem):
     rows, columns = out_ref.shape[:2]
     span = pl.ds(bounds[1], columns - bounds[1])
+    _, has = neighbours(counts)
     run(
         [
-            pltpu.make_async_copy(last_ref.at[place], out_ref.at[row, span], sem.at[place])
+            (
+                pltpu.make_async_copy(last_ref.at[place], out_ref.at[row, span], sem.at[place]),
+                jnp.logical_and(jnp.logical_not(late()), has[0][place]),
+            )
             for place, row in enumerate((0, rows - 1))
-        ],
-        jnp.logical_not(late()),
+        ]
     )
 
 
@@ -467,7 +452,7 @@
             ),
         )(pressure, earlier, speed_square)
         out, token = pl.pallas_call(
-            functools.partial(write_kernel, bounds),
+            functools.partial(write_kernel, counts, bounds),
             out_shape=(pltpu.HBM(pressure.shape, jnp.float32), pltpu.VMEM((8, 128), jnp.float32)),
             in_specs=[vmem],
             out_specs=(hbm, vmem),
@@ -489,7 +474,7 @@
             ),
         )(end, edges, paces, token)
         return pl.pallas_call(
-            functools.partial(patch_kernel, bounds),
+            functools.partial(patch_kernel, counts, bounds),
             out_shape=pltpu.HBM(pressure.shape, jnp.float32),
             in_specs=[hbm, vmem],
             out_specs=hbm,

time: 185 us -> 185 us (level)
  no operation moved by 1% of the time
where the time goes in v4:
time: 185 us
  Pallas kernels  185 us (100%)
    pallas_call x1, Pallas kernels, shards(): pl.pallas_call(functools.partial(main_kernel, counts, bounds, early_first...  168 us
    pallas_call x1, Pallas kernels, shards(): pl.pallas_call(functools.partial(tail_kernel, counts, pieces), out_shape=...  13 us

profile of v4, /device:TPU:1, one launch (start us, length us, event | category | flops | bytes accessed | tf_op | source)
XLA Modules:
  0.0 184.8 jit_solution(6803750089200703093)
XLA Ops:
  0.0 167.7 %shard_map.37 = (f32[4,64,64,128]{3,2,1,0:T(8,128)S(1)}, f32[2,20,64,128]{3,2,1,0:T(8,128)S(1)}, f32[2,20,64,128]{3,2,1,0:T(8,128)S(1)}) custom-call(f32[4,64,64,128]{3,2,1,0:T(8,128)} %start_ref.1, f32[4,64,64,128]{3,2,1,0:T(8,128)} %earlier_ref.1, f32[4,64,64,128]{3,2,1,0:T(8,128)} %speed_ref.1), custom_call_target="tpu_custom_call" | custom-call | tf_op jit(solution)/shard_map/pallas_call | solution.py:434
  167.7 3.2 %shard_map.38 = (f32[4,64,64,128]{3,2,1,0:T(8,128)}, f32[8,128]{1,0:T(8,128)S(1)}) custom-call(f32[4,64,64,128]{3,2,1,0:T(8,128)S(1)} %get-tuple-element.10.end_ref), custom_call_target="tpu_custom_call" | custom-call | tf_op jit(solution)/shard_map/pallas_call | solution.py:454
  170.8 13.0 %shard_map.39.last_ref = f32[2,20,64,128]{3,2,1,0:T(8,128)S(1)} custom-call(f32[4,64,64,128]{3,2,1,0:T(8,128)S(1)} %get-tuple-element.10.end_ref, f32[2,20,64,128]{3,2,1,0:T(8,128)S(1)} %get-tuple-element.12.edge_ref, f32[2,20,64,128]{3,2,1,0:T(8,128)S(1)} %get-tuple-element.13.pace_ref, f32[8,128]{1,0:T(8,128)S(1)} %get-tuple-element.14.token_ref), custom_call_target="tpu_custom_call" | custom-call | tf_op jit(solution)/shard_map/pallas_call | solution.py:462
  183.9 0.9 shard_map.40

commit v5 on v4

--- a/solution.py
+++ b/solution.py
@@ -8,8 +8,8 @@
 from jax.sharding import PartitionSpec as P
 
 STEPS = 4
-TAIL = 20
-EARLY = 4
+TAIL = 16
+EARLY = 2
 END = 2
 PAD = 8
 AXES = ("lat", "lon", "lev")
@@ -308,12 +308,12 @@
                         edge_ref[place, x - 1 - split] = later
                         pace_ref[place, x - 1 - split] = speed[y - 1, x - 1]
 
-            lat_each(step + 1, part, "start")
-
             @pl.loop(first + 1, first + width + 1)
             def _(x):
                 for y in range(2, rows):
                     other[y, x, inside] = advance(step, y, x)
+
+            lat_each(step + 1, part, "start")
 
         side_each(step + 1, "start")
 

time: 185 us -> 185 us (level)
    pallas_call x1, Pallas kernels: 13 us -> 10.2 us  [shards(): pl.pallas_call(functools.partial(tail_kernel, counts, pieces), out_shape=...]
    pallas_call x1, Pallas kernels: 168 us -> 170 us  [shards(): pl.pallas_call(functools.partial(main_kernel, counts, bounds, early_first...]
where the time goes in v5:
time: 185 us
  Pallas kernels  185 us (100%)
    pallas_call x1, Pallas kernels, shards(): pl.pallas_call(functools.partial(main_kernel, counts, bounds, early_first...  170 us
    pallas_call x1, Pallas kernels, shards(): pl.pallas_call(functools.partial(tail_kernel, counts, pieces), out_shape=...  10.2 us

profile of v5, /device:TPU:1, one launch (start us, length us, event | category | flops | bytes accessed | tf_op | source)
XLA Modules:
  0.0 184.6 jit_solution(10350105244999129389)
XLA Ops:
  0.0 170.3 %shard_map.37 = (f32[4,64,64,128]{3,2,1,0:T(8,128)S(1)}, f32[2,16,64,128]{3,2,1,0:T(8,128)S(1)}, f32[2,16,64,128]{3,2,1,0:T(8,128)S(1)}) custom-call(f32[4,64,64,128]{3,2,1,0:T(8,128)} %start_ref.1, f32[4,64,64,128]{3,2,1,0:T(8,128)} %earlier_ref.1, f32[4,64,64,128]{3,2,1,0:T(8,128)} %speed_ref.1), custom_call_target="tpu_custom_call" | custom-call | tf_op jit(solution)/shard_map/pallas_call | solution.py:434
  170.3 3.2 %shard_map.38 = (f32[4,64,64,128]{3,2,1,0:T(8,128)}, f32[8,128]{1,0:T(8,128)S(1)}) custom-call(f32[4,64,64,128]{3,2,1,0:T(8,128)S(1)} %get-tuple-element.10.end_ref), custom_call_target="tpu_custom_call" | custom-call | tf_op jit(solution)/shard_map/pallas_call | solution.py:454
  173.6 10.2 %shard_map.39.last_ref = f32[2,16,64,128]{3,2,1,0:T(8,128)S(1)} custom-call(f32[4,64,64,128]{3,2,1,0:T(8,128)S(1)} %get-tuple-element.10.end_ref, f32[2,16,64,128]{3,2,1,0:T(8,128)S(1)} %get-tuple-element.12.edge_ref, f32[2,16,64,128]{3,2,1,0:T(8,128)S(1)} %get-tuple-element.13.pace_ref, f32[8,128]{1,0:T(8,128)S(1)} %get-tuple-element.14.token_ref), custom_call_target="tpu_custom_call" | custom-call | tf_op jit(solution)/shard_map/pallas_call | solution.py:462
  183.8 0.8 shard_map.40

commit v6 on v5

--- a/solution.py
+++ b/solution.py
@@ -8,9 +8,9 @@
 from jax.sharding import PartitionSpec as P
 
 STEPS = 4
-TAIL = 16
+TAIL = 14
 EARLY = 2
-END = 2
+END = 1
 PAD = 8
 AXES = ("lat", "lon", "lev")
 MESH = pl.DeviceIdType.MESH
@@ -111,8 +111,8 @@
             )
         )
     loads = [
-        pltpu.make_async_copy(earlier_ref, odd.at[pl.ds(1, rows), pl.ds(1, columns), inside], load_sem.at[4]),
-        pltpu.make_async_copy(speed_ref, speed, load_sem.at[5]),
+        pltpu.make_async_copy(earlier_ref, odd.at[pl.ds(1, rows), pl.ds(1, columns), inside], load_sem.at[0]),
+        pltpu.make_async_copy(speed_ref, speed, load_sem.at[1]),
     ]
     behind = late()
     ahead = jnp.logical_not(behind)
@@ -440,7 +440,7 @@
                 field,
                 field,
                 pltpu.VMEM(pressure.shape, jnp.float32),
-                dma((6,)),
+                dma((4,)),
                 dma((2, parts)),
                 dma((2, 2, parts)),
                 dma((2, 2)),

time: 185 us -> 185 us (level)
  no operation moved by 1% of the time
where the time goes in v6:
time: 185 us
  Pallas kernels  185 us (100%)
    pallas_call x1, Pallas kernels, shards(): pl.pallas_call(functools.partial(main_kernel, counts, bounds, early_first...  172 us
    pallas_call x1, Pallas kernels, shards(): pl.pallas_call(functools.partial(tail_kernel, counts, pieces), out_shape=...  8.78 us

profile of v6, /device:TPU:1, one launch (start us, length us, event | category | flops | bytes accessed | tf_op | source)
XLA Modules:
  0.0 184.6 jit_solution(15657254130231108308)
XLA Ops:
  0.0 171.8 %shard_map.37 = (f32[4,64,64,128]{3,2,1,0:T(8,128)S(1)}, f32[2,14,64,128]{3,2,1,0:T(8,128)S(1)}, f32[2,14,64,128]{3,2,1,0:T(8,128)S(1)}) custom-call(f32[4,64,64,128]{3,2,1,0:T(8,128)} %start_ref.1, f32[4,64,64,128]{3,2,1,0:T(8,128)} %earlier_ref.1, f32[4,64,64,128]{3,2,1,0:T(8,128)} %speed_ref.1), custom_call_target="tpu_custom_call" | custom-call | tf_op jit(solution)/shard_map/pallas_call | solution.py:434
  171.8 3.2 %shard_map.38 = (f32[4,64,64,128]{3,2,1,0:T(8,128)}, f32[8,128]{1,0:T(8,128)S(1)}) custom-call(f32[4,64,64,128]{3,2,1,0:T(8,128)S(1)} %get-tuple-element.10.end_ref), custom_call_target="tpu_custom_call" | custom-call | tf_op jit(solution)/shard_map/pallas_call | solution.py:454
  175.0 8.8 %shard_map.39.last_ref = f32[2,14,64,128]{3,2,1,0:T(8,128)S(1)} custom-call(f32[4,64,64,128]{3,2,1,0:T(8,128)S(1)} %get-tuple-element.10.end_ref, f32[2,14,64,128]{3,2,1,0:T(8,128)S(1)} %get-tuple-element.12.edge_ref, f32[2,14,64,128]{3,2,1,0:T(8,128)S(1)} %get-tuple-element.13.pace_ref, f32[8,128]{1,0:T(8,128)S(1)} %get-tuple-element.14.token_ref), custom_call_target="tpu_custom_call" | custom-call | tf_op jit(solution)/shard_map/pallas_call | solution.py:462
  183.8 0.8 shard_map.40

commit v7 on v6

--- a/solution.py
+++ b/solution.py
@@ -8,9 +8,9 @@
 from jax.sharding import PartitionSpec as P
 
 STEPS = 4
-TAIL = 14
+TAIL = 18
 EARLY = 2
-END = 1
+END = 2
 PAD = 8
 AXES = ("lat", "lon", "lev")
 MESH = pl.DeviceIdType.MESH

time: 185 us -> 185 us (level)
    pallas_call x1, Pallas kernels: 8.78 us -> 11.7 us  [shards(): pl.pallas_call(functools.partial(tail_kernel, counts, pieces), out_shape=...]
    pallas_call x1, Pallas kernels: 172 us -> 169 us  [shards(): pl.pallas_call(functools.partial(main_kernel, counts, bounds, early_first...]
where the time goes in v7:
time: 185 us
  Pallas kernels  185 us (100%)
    pallas_call x1, Pallas kernels, shards(): pl.pallas_call(functools.partial(main_kernel, counts, bounds, early_first...  169 us
    pallas_call x1, Pallas kernels, shards(): pl.pallas_call(functools.partial(tail_kernel, counts, pieces), out_shape=...  11.7 us

profile of v7, /device:TPU:1, one launch (start us, length us, event | category | flops | bytes accessed | tf_op | source)
XLA Modules:
  0.0 184.6 jit_solution(6069226820699712329)
XLA Ops:
  0.0 168.9 %shard_map.37 = (f32[4,64,64,128]{3,2,1,0:T(8,128)S(1)}, f32[2,18,64,128]{3,2,1,0:T(8,128)S(1)}, f32[2,18,64,128]{3,2,1,0:T(8,128)S(1)}) custom-call(f32[4,64,64,128]{3,2,1,0:T(8,128)} %start_ref.1, f32[4,64,64,128]{3,2,1,0:T(8,128)} %earlier_ref.1, f32[4,64,64,128]{3,2,1,0:T(8,128)} %speed_ref.1), custom_call_target="tpu_custom_call" | custom-call | tf_op jit(solution)/shard_map/pallas_call | solution.py:434
  168.9 3.2 %shard_map.38 = (f32[4,64,64,128]{3,2,1,0:T(8,128)}, f32[8,128]{1,0:T(8,128)S(1)}) custom-call(f32[4,64,64,128]{3,2,1,0:T(8,128)S(1)} %get-tuple-element.10.end_ref), custom_call_target="tpu_custom_call" | custom-call | tf_op jit(solution)/shard_map/pallas_call | solution.py:454
  172.1 11.7 %shard_map.39.last_ref = f32[2,18,64,128]{3,2,1,0:T(8,128)S(1)} custom-call(f32[4,64,64,128]{3,2,1,0:T(8,128)S(1)} %get-tuple-element.10.end_ref, f32[2,18,64,128]{3,2,1,0:T(8,128)S(1)} %get-tuple-element.12.edge_ref, f32[2,18,64,128]{3,2,1,0:T(8,128)S(1)} %get-tuple-element.13.pace_ref, f32[8,128]{1,0:T(8,128)S(1)} %get-tuple-element.14.token_ref), custom_call_target="tpu_custom_call" | custom-call | tf_op jit(solution)/shard_map/pallas_call | solution.py:462
  183.8 0.8 shard_map.40
